TPU v7x, 768 devices: a whole 4x8x12 slice. The times are simulated.
768 devices in a mesh: pp: 12 (over z), tp: 16 (over y, core), ep: 4 (over x).
Axes of the slice: x: 4, y: 8, z: 12, core: 2. Of those that a mesh axis runs over, the one named last changes fastest.
Arguments:
- incoming: bfloat16 [12, 8192, 2048], P('pp', ('tp', 'ep')), may hold values from -6 to 6
- expert_ids: int32 [12, 8192, 2], P('pp', ('tp', 'ep')), may hold values from 0 to 63, all different within a row; in each aligned block of 128 rows (0 to 127, 128 to 255, ..., all dimensions but the last counted through in order) at most 8 rows name the same one
- gate_scores: float32 [12, 8192, 2], P('pp', ('tp', 'ep')), may hold values from 0.05 to 1
- gate_proj: bfloat16 [64, 2048, 768], P(('tp', 'ep')), may hold values from -0.125 to 0.125
- up_proj: bfloat16 [64, 2048, 768], P(('tp', 'ep')), may hold values from -0.125 to 0.125
- down_proj: bfloat16 [64, 768, 2048], P(('tp', 'ep')), may hold values from -0.21875 to 0.21875
Outputs:
- combined: bfloat16 [12, 8192, 2048], P('pp', ('tp', 'ep'))
Inputs may be any that keep to these rules, and one draw needn't show every extreme that they name: `expert_ids`: each token names 2 different experts. Among the tokens of one device of one section no expert is named more than 8 times, and in every draw some device's tokens name one expert exactly 8 times.
All inputs are finite; a program needn't handle non-finite values.
Results may differ from a plain program's by a relative error of at most 0.0045.
Values may be sent and summed in bfloat16 or wider, within the bound.
No kernel may reach another device: no remote copies, remote signals or barrier semaphores. Data moves between devices by JAX's collectives and lax.ppermute only.
A program may use at most 64 MiB of HBM per device.

v0:
```python
import jax
import jax.numpy as jnp
from jax import lax
from jax.sharding import PartitionSpec as P


def shifted(block, axis, distance):
    devices = range(lax.axis_size(axis))
    route = [((i - distance) % len(devices), i) for i in devices]
    return lax.ppermute(block, axis, route)


def expert_apply(tokens_in, gate_mat, up_mat, down_mat):
    gate_part = jnp.dot(tokens_in, gate_mat, preferred_element_type=jnp.float32)
    upward = jnp.dot(tokens_in, up_mat, preferred_element_type=jnp.float32)
    hidden = (jax.nn.silu(gate_part) * upward).astype(jnp.bfloat16)
    return jnp.dot(hidden, down_mat, preferred_element_type=jnp.float32).astype(jnp.bfloat16)


def shards(incoming, expert_ids, gate_scores, gate_proj, up_proj, down_proj):
    arrived = shifted(incoming, "pp", 1)[0]
    tok_count, features = arrived.shape
    top_count = expert_ids.shape[2]
    expert_count = lax.axis_size("tp") * lax.axis_size("ep")
    capacity = min(tok_count, 2 * tok_count * top_count // expert_count)
    values = arrived.astype(jnp.float32)
    normed = (values * lax.rsqrt(jnp.mean(values * values, axis=1, keepdims=True) + 1e-06)).astype(
        jnp.bfloat16
    )
    chosen = expert_ids[0].reshape(-1)
    onehot = (chosen[:, None] == jnp.arange(expert_count, dtype=jnp.int32)[None, :]).astype(
        jnp.int32
    )
    before = jnp.cumsum(onehot, axis=0) - onehot
    slot_of = jnp.sum(before * onehot, axis=1)
    destination = chosen * capacity + slot_of
    owner_row = jnp.arange(chosen.shape[0], dtype=jnp.int32) // top_count
    source_row = (
        jnp.full((expert_count * capacity,), tok_count, jnp.int32).at[destination].set(owner_row)
    )
    occupied = jnp.zeros((expert_count * capacity,), jnp.int32).at[destination].set(1)
    with_blank = jnp.concatenate([normed, jnp.zeros((1, features), jnp.bfloat16)], axis=0)
    outgoing = with_blank[source_row].reshape(expert_count, capacity, features)
    occupied = occupied.reshape(expert_count, capacity)
    gate_mat, up_mat, down_mat = (gate_proj[0], up_proj[0], down_proj[0])
    received_rows = lax.all_to_all(outgoing, ("tp", "ep"), split_axis=0, concat_axis=0, tiled=True)
    flat_rows = received_rows.reshape(-1, features)
    flat_live = lax.all_to_all(
        occupied, ("tp", "ep"), split_axis=0, concat_axis=0, tiled=True
    ).reshape(-1)
    answered = expert_apply(flat_rows, gate_mat, up_mat, down_mat) * flat_live[:, None].astype(
        jnp.bfloat16
    )
    answered = answered.reshape(received_rows.shape)
    returned = lax.all_to_all(answered, ("tp", "ep"), split_axis=0, concat_axis=0, tiled=True)
    picked = returned.reshape(expert_count * capacity, features)[destination].reshape(
        tok_count, top_count, features
    )
    scores = gate_scores[0]
    weights = scores / jnp.sum(scores, axis=1, keepdims=True)
    combined = values + jnp.sum(weights[:, :, None] * picked.astype(jnp.float32), axis=1)
    return combined.astype(jnp.bfloat16)[None]


def solution(mesh):
    placed = (
        P("pp", ("tp", "ep"), None),
        P("pp", ("tp", "ep"), None),
        P("pp", ("tp", "ep"), None),
        P(("tp", "ep"), None, None),
        P(("tp", "ep"), None, None),
        P(("tp", "ep"), None, None),
    )
    return jax.shard_map(
        shards, mesh=mesh, in_specs=placed, out_specs=P("pp", ("tp", "ep"), None), check_vma=False
    )
```

profile of v0, /device:TPU:2, one launch (start us, length us, event | category | flops | bytes accessed | tf_op | source)
XLA Modules:
  0.0 185.0 jit_solution(9658520421589710183)
XLA Ops:
  0.0 4.5 %collective-permute-start = (bf16[1,128,2048]{2,1,0:T(8,128)(2,1)}, bf16[1,128,2048]{2,1,0:T(8,128)(2,1)}, u32[]{:S(2)}, u32[]{:S(2)}) collective-permute-start(bf16[1,128,2048]{2,1,0:T(8,128)(2,1)} %param.6), channel_id=1, source_target_pairs={{704,0},{0,64},{64,128},{128,192},{192,256},{256,320},{320,384},{3... | collective-permute-start | bytes 1572872 | tf_op jit(solution)/shard_map/ppermute | solution.py:10
  4.5 0.8 copy.15
  5.6 0.7 broadcast_multiply_fusion
  6.3 0.6 reduce-window.6
  6.9 0.2 slice_reduce_fusion
  7.5 1.4 scatter_custom_fusion.1
  8.9 0.7 all_to_all.13
  9.6 11.2 %all-to-all-start.1 = ((s32[64,1,8]{2,1,0:T(1,128)}), s32[64,1,8]{2,1,0:T(1,128)S(1)}, u32[]{:S(2)}, u32[]{:S(2)}) async-start(s32[64,1,8]{2,1,0:T(1,128)} %bitcast.10), calls=%async_computation.1 | async-start | bytes 65536 | tf_op jit(solution)/shard_map/all_to_all | solution.py:48
  20.8 1.4 scatter_custom_fusion
  22.3 4.8 %collective-permute-done = bf16[1,128,2048]{2,1,0:T(8,128)(2,1)} collective-permute-done((bf16[1,128,2048]{2,1,0:T(8,128)(2,1)}, bf16[1,128,2048]{2,1,0:T(8,128)(2,1)}, u32[]{:S(2)}, u32[]{:S(2)}) %collective-permute-start) | collective-permute-done | bytes 524320 | tf_op jit(solution)/shard_map/ppermute | solution.py:10
  27.1 1.2 fusion.23
  28.3 1.2 fusion.24
  29.5 0.8 concatenate.3
  30.4 6.4 %gather_fusion = bf16[512,2048]{1,0:T(8,128)(2,1)} fusion(bf16[129,2048]{1,0:T(8,128)(2,1)} %concatenate.3, s32[1024]{0:T(1024)S(1)} %pad_clamp_fusion.1), kind=kCustom, calls=%fused_computation | custom fusion | bytes 4196352 | tf_op jit(solution)/shard_map/gather | solution.py:43
  36.7 10.8 %all-to-all-start = ((bf16[64,8,2048]{2,1,0:T(8,128)(2,1)}), bf16[64,8,2048]{2,1,0:T(8,128)(2,1)}, u32[]{:S(2)}, u32[]{:S(2)}) async-start(bf16[64,8,2048]{2,1,0:T(8,128)(2,1)} %bitcast.68), calls=%async_computation | async-start | bytes 4194304 | tf_op jit(solution)/shard_map/all_to_all | solution.py:46
  47.8 51.0 %all-to-all-done = bf16[64,8,2048]{2,1,0:T(8,128)(2,1)} async-done(((bf16[64,8,2048]{2,1,0:T(8,128)(2,1)}), bf16[64,8,2048]{2,1,0:T(8,128)(2,1)}, u32[]{:S(2)}, u32[]{:S(2)}) %all-to-all-start) | async-done | bytes 2097184 | tf_op jit(solution)/shard_map/all_to_all | solution.py:46
  98.7 5.5 %fusion.4 = f32[512,768]{1,0:T(8,128)} fusion(bf16[1,2048,768]{2,1,0:T(8,128)(2,1)} %param.9, bf16[64,8,2048]{2,1,0:T(8,128)(2,1)} %all-to-all-done), kind=kOutput, calls=%fused_computation.8 | convolution fusion | flops 1610612736 | bytes 6815744 | tf_op jit(solution)/shard_map/dot_general | solution.py:14
  104.2 8.2 %fusion.12 = bf16[64,8,2048]{2,1,0:T(8,128)(2,1)} fusion(bf16[1,768,2048]{2,1,0:T(8,128)(2,1)S(1)} %copy-done, bf16[512]{0:T(512)(128)(2,1)S(1)} %convert_element_type.55, f32[512,768]{1,0:T(8,128)} %fusion.4, bf16[1,2048,768]{2,1,0:T(8,128)(2,1)} %param.10, bf16[64,8,2048]{2,1,0:T(8,128)(2,1)} %all-to-all-done), kind=kOutput, calls=%fused_computation.12 | convolution fusion | flops 3228827648 | bytes 12059648 | tf_op jit(solution)/shard_map/dot_general | solution.py:17
  112.5 5.9 %all-to-all-start.2 = ((bf16[64,8,2048]{2,1,0:T(8,128)(2,1)}), bf16[64,8,2048]{2,1,0:T(8,128)(2,1)}, u32[]{:S(2)}, u32[]{:S(2)}) async-start(bf16[64,8,2048]{2,1,0:T(8,128)(2,1)} %fusion.12), calls=%async_computation.2 | async-start | bytes 4194304 | tf_op jit(solution)/shard_map/all_to_all | solution.py:55
  118.6 51.0 %all-to-all-done.2 = bf16[64,8,2048]{2,1,0:T(8,128)(2,1)} async-done(((bf16[64,8,2048]{2,1,0:T(8,128)(2,1)}), bf16[64,8,2048]{2,1,0:T(8,128)(2,1)}, u32[]{:S(2)}, u32[]{:S(2)}) %all-to-all-start.2) | async-done | bytes 2097184 | tf_op jit(solution)/shard_map/all_to_all | solution.py:55
  169.6 5.2 %gather_fusion.1 = bf16[256,2048]{1,0:T(8,128)(2,1)} fusion(bf16[512,2048]{1,0:T(8,128)(2,1)} %bitcast.12, s32[1024]{0:T(1024)S(1)} %pad_clamp_fusion), kind=kCustom, calls=%fused_computation.1 | custom fusion | bytes 2098176 | tf_op jit(solution)/shard_map/gather | solution.py:56
  174.8 3.4 %reshape.110 = f32[128,2,2048]{2,1,0:T(2,128)} reshape(bf16[256,2048]{1,0:T(8,128)(2,1)} %gather_fusion.1) | data formatting | bytes 3145728 | tf_op jit(solution)/shard_map/convert_element_type | solution.py:61
  178.2 4.8 %multiply_reduce_fusion = f32[128,2048]{1,0:T(8,128)S(1)} fusion(f32[128,2,2048]{2,1,0:T(2,128)} %reshape.110, f32[128,2]{1,0:T(8,128)S(1)} %copy.13), kind=kLoop, calls=%fused_computation.15 | loop fusion | flops 786432 | bytes 3146752 | tf_op jit(solution)/shard_map/reduce_sum | solution.py:61
  183.0 2.0 %fusion.25 = bf16[1,128,2048]{2,1,0:T(8,128)(2,1)} fusion(bf16[1,128,2048]{2,1,0:T(8,128)(2,1)} %collective-permute-done, f32[128,2048]{1,0:T(8,128)S(1)} %multiply_reduce_fusion), kind=kLoop, calls=%fused_computation.23 | loop fusion | flops 786432 | bytes 2097152 | tf_op jit(solution)/shard_map/convert_element_type | solution.py:62
  (25 shorter events, 1.1 us)
Async XLA Ops:
  0.0 104.2 %copy-start = (bf16[1,768,2048]{2,1,0:T(8,128)(2,1)S(1)}, bf16[1,768,2048]{2,1,0:T(8,128)(2,1)}, u32[]{:S(2)}) copy-start(bf16[1,768,2048]{2,1,0:T(8,128)(2,1)} %param.11) | copy-start | bytes 9437188
  0.0 27.1 %collective-permute-start = (bf16[1,128,2048]{2,1,0:T(8,128)(2,1)}, bf16[1,128,2048]{2,1,0:T(8,128)(2,1)}, u32[]{:S(2)}, u32[]{:S(2)}) collective-permute-start(bf16[1,128,2048]{2,1,0:T(8,128)(2,1)} %param.6), channel_id=1, source_target_pairs={{704,0},{0,64},{64,128},{128,192},{192,256},{256,320},{320,384},{3... | collective-permute-start | bytes 1572872 | tf_op jit(solution)/shard_map/ppermute | solution.py:10
  9.6 27.1 %all-to-all-start.1 = ((s32[64,1,8]{2,1,0:T(1,128)}), s32[64,1,8]{2,1,0:T(1,128)S(1)}, u32[]{:S(2)}, u32[]{:S(2)}) async-start(s32[64,1,8]{2,1,0:T(1,128)} %bitcast.10), calls=%async_computation.1 | async-start | bytes 65536 | tf_op jit(solution)/shard_map/all_to_all | solution.py:48
  36.7 62.0 %all-to-all-start = ((bf16[64,8,2048]{2,1,0:T(8,128)(2,1)}), bf16[64,8,2048]{2,1,0:T(8,128)(2,1)}, u32[]{:S(2)}, u32[]{:S(2)}) async-start(bf16[64,8,2048]{2,1,0:T(8,128)(2,1)} %bitcast.68), calls=%async_computation | async-start | bytes 4194304 | tf_op jit(solution)/shard_map/all_to_all | solution.py:46
  112.5 5.9 %copy-start.1 = (f32[1,128,2]{1,2,0:T(2,128)S(1)}, f32[1,128,2]{1,2,0:T(2,128)}, u32[]{:S(2)}) copy-start(f32[1,128,2]{1,2,0:T(2,128)} %param.8) | copy-start | bytes 3076
  112.5 57.1 %all-to-all-start.2 = ((bf16[64,8,2048]{2,1,0:T(8,128)(2,1)}), bf16[64,8,2048]{2,1,0:T(8,128)(2,1)}, u32[]{:S(2)}, u32[]{:S(2)}) async-start(bf16[64,8,2048]{2,1,0:T(8,128)(2,1)} %fusion.12), calls=%async_computation.2 | async-start | bytes 4194304 | tf_op jit(solution)/shard_map/all_to_all | solution.py:55
where the time goes:
time: 186 us; the launch traced here: 185 us
  waiting for transfers between devices  107 us (58%)
  starting transfers between devices  32.5 us (17%)
  local copies, waits for them, and re-layouts  21 us (11%)
  matrix products  13.7 us (7%)
  other arithmetic  10.8 us (6%)
    all_to_all x1, waiting for transfers between devices, shards(): lax.all_to_all(answered, ('tp', 'ep'), split_axis=0, concat_axis=0, tiled...  51 us
    all_to_all x1, waiting for transfers between devices, shards(): lax.all_to_all(outgoing, ('tp', 'ep'), split_axis=0, concat_axis=0, tiled...  51 us
    all_to_all x1, starting transfers between devices, shards(): lax.all_to_all(occupied, ('tp', 'ep'), split_axis=0, concat_axis=0, tiled...  11.2 us
    all_to_all x1, starting transfers between devices, shards(): lax.all_to_all(outgoing, ('tp', 'ep'), split_axis=0, concat_axis=0, tiled...  10.8 us
    dot_general x1, matrix products, expert_apply(): jnp.dot(hidden, down_mat, preferred_element_type=jnp.float32)  8.23 us
    gather x1, local copies, waits for them, and re-layouts, shards(): outgoing = with_blank[source_row].reshape(expert_count, capacity, features)  6.36 us
    all_to_all x1, starting transfers between devices, shards(): lax.all_to_all(answered, ('tp', 'ep'), split_axis=0, concat_axis=0, tiled...  5.93 us
    dot_general x1, matrix products, expert_apply(): gate_part = jnp.dot(tokens_in, gate_mat, preferred_element_type=jnp.float32)  5.48 us
  transfers between devices with their start and end apart: 4, of which 3 were waited for; matrix products, arithmetic and copies ran while one was open for 9% of the time, Pallas kernels for 0%

commit v1 on v0

v1 whole, which is shorter than its diff:
```python
import functools

import jax
import jax.numpy as jnp
from jax import lax
from jax.experimental import pallas as pl
from jax.experimental.pallas import tpu as pltpu
from jax.sharding import PartitionSpec as P

CHUNKS = 1
AXES = ("tp", "ep")
F32, BF16, I32 = jnp.float32, jnp.bfloat16, jnp.int32


def shifted(block, axis, distance):
    devices = range(lax.axis_size(axis))
    route = [((i - distance) % len(devices), i) for i in devices]
    return lax.ppermute(block, axis, route)


def iota(shape, dim):
    return lax.broadcasted_iota(I32, shape, dim)


def dispatch_kernel(experts, cap, ids_ref, x_ref, *refs):
    out_refs, normed_ref = refs[:-1], refs[-1]
    step = pl.program_id(0)

    @pl.when(step == 0)
    def _():
        values = x_ref[...].astype(F32)
        scale = lax.rsqrt(jnp.mean(values * values, axis=1, keepdims=True) + 1e-06)
        normed_ref[...] = (values * scale).astype(BF16)

    ids = ids_ref[...]
    tokens = ids.shape[1]
    named = ids[0:1, :] * 0 + step * experts + iota((experts, tokens), 0)
    member = (ids[0:1, :] == named) | (ids[1:2, :] == named)
    earlier = (iota((tokens, tokens), 0) < iota((tokens, tokens), 1)).astype(BF16)
    slot = jnp.dot(member.astype(BF16), earlier, preferred_element_type=F32).astype(I32)
    slot = jnp.where(member, slot, -1)
    pick = slot[:, None, :] == iota((experts, cap, tokens), 1)
    pick = pick.astype(F32).reshape(experts * cap, tokens).astype(BF16)
    width = out_refs[0].shape[1]
    for c, out_ref in enumerate(out_refs):
        rows = normed_ref[:, c * width : (c + 1) * width]
        out_ref[...] = jnp.dot(pick, rows, preferred_element_type=F32).astype(BF16)


def dispatch(ids, arrived, experts, cap, chunks, steps=4):
    tokens, features = arrived.shape
    width = features // chunks
    rows = experts * cap // steps
    return pl.pallas_call(
        functools.partial(dispatch_kernel, experts // steps, cap),
        grid=(steps,),
        in_specs=[
            pl.BlockSpec(ids.shape, lambda i: (0, 0)),
            pl.BlockSpec(arrived.shape, lambda i: (0, 0)),
        ],
        out_specs=[pl.BlockSpec((rows, width), lambda i: (i, 0))] * chunks,
        out_shape=[jax.ShapeDtypeStruct((experts * cap, width), BF16)] * chunks,
        scratch_shapes=[pltpu.VMEM((tokens, features), BF16)],
        name="dispatch",
    )(ids, arrived)


def combine_kernel(experts, cap, ids_ref, scores_ref, back_ref, x_ref, *refs):
    out_ref, pick_ref, weight_ref = refs[-3:]
    tokens = ids_ref.shape[1]
    square = (tokens, tokens)

    @pl.when(pl.program_id(0) == 0)
    def _():
        scores = scores_ref[...]
        weights = scores / jnp.sum(scores, axis=0, keepdims=True)
        ids = ids_ref[...].astype(F32)
        column = lambda a, k: jnp.transpose(jnp.broadcast_to(a[k : k + 1, :], square))
        names = [column(ids, k).astype(I32) for k in range(2)]
        lane = iota(square, 1)
        member = ((names[0] == lane) | (names[1] == lane)).astype(BF16)
        earlier = (iota(square, 1) < iota(square, 0)).astype(BF16)
        slot = jnp.dot(earlier, member, preferred_element_type=F32)
        for k in range(2):
            mine = jnp.sum(jnp.where(names[k] == lane, slot, 0.0), axis=1, keepdims=True)
            at = names[k][:, 0:1] * cap + mine.astype(I32)
            here = (iota((tokens, experts * cap), 1) == at).astype(BF16)
            pick_ref[k * tokens : (k + 1) * tokens, :] = here
            weight_ref[k * tokens : (k + 1) * tokens, :] = column(weights, k)

    picked = jnp.dot(pick_ref[...], back_ref[...], preferred_element_type=F32)
    picked = picked * weight_ref[:, 0:1]
    total = x_ref[...].astype(F32) + (picked[:tokens] + picked[tokens:])
    out_ref[...] = total.astype(BF16)


def combine(ids, scores, back, arrived, out, chunk, experts, cap, block=512):
    tokens, features = arrived.shape
    width = back.shape[1]
    base = chunk * width // block
    small = pl.BlockSpec(ids.shape, lambda i: (0, 0))
    place = pl.BlockSpec((tokens, block), lambda i: (0, base + i))
    operands = [ids, scores, back, arrived]
    specs = [small, small, pl.BlockSpec((experts * cap, block), lambda i: (0, i)), place]
    aliases = {}
    if out is not None:
        operands.append(out)
        specs.append(pl.BlockSpec(memory_space=pl.ANY))
        aliases = {4: 0}
    return pl.pallas_call(
        functools.partial(combine_kernel, experts, cap),
        grid=(width // block,),
        in_specs=specs,
        out_specs=place,
        out_shape=jax.ShapeDtypeStruct((tokens, features), BF16),
        scratch_shapes=[
            pltpu.VMEM((2 * tokens, experts * cap), BF16),
            pltpu.VMEM((2 * tokens, tokens), F32),
        ],
        input_output_aliases=aliases,
        name="combine",
    )(*operands)


def exchange(block, experts):
    shape = block.shape
    block = block.reshape(experts, -1, shape[1])
    block = lax.all_to_all(block, AXES, split_axis=0, concat_axis=0, tiled=True)
    return block.reshape(shape)


def shards(incoming, expert_ids, gate_scores, gate_proj, up_proj, down_proj):
    arrived = shifted(incoming, "pp", 1)[0]
    tokens, features = arrived.shape
    experts = lax.axis_size("tp") * lax.axis_size("ep")
    cap = min(tokens, 2 * tokens * expert_ids.shape[2] // experts)
    ids, scores = expert_ids[0].T, gate_scores[0].T
    width = features // CHUNKS
    outgoing = dispatch(ids, arrived, experts, cap, CHUNKS)
    gate = up = 0.0
    for c, block in enumerate(outgoing):
        rows = exchange(block, experts)
        part = slice(c * width, (c + 1) * width)
        gate = gate + jnp.dot(rows, gate_proj[0, part], preferred_element_type=F32)
        up = up + jnp.dot(rows, up_proj[0, part], preferred_element_type=F32)
    hidden = (jax.nn.silu(gate) * up).astype(BF16)
    out = None
    backs = []
    for c in range(CHUNKS):
        part = slice(c * width, (c + 1) * width)
        answered = jnp.dot(hidden, down_proj[0, :, part], preferred_element_type=F32)
        backs.append(exchange(answered.astype(BF16), experts))
    for c, back in enumerate(backs):
        out = combine(ids, scores, back, arrived, out, c, experts, cap)
    return out[None]


def solution(mesh):
    placed = (
        P("pp", ("tp", "ep"), None),
        P("pp", ("tp", "ep"), None),
        P("pp", ("tp", "ep"), None),
        P(("tp", "ep"), None, None),
        P(("tp", "ep"), None, None),
        P(("tp", "ep"), None, None),
    )
    return jax.shard_map(
        shards, mesh=mesh, in_specs=placed, out_specs=P("pp", ("tp", "ep"), None), check_vma=False
    )
```

time: 186 us -> 168 us (0.903)
  blocking collectives: 0 us -> 119 us
  waiting for transfers between devices: 107 us -> 22.5 us
  starting transfers between devices: 32.5 us -> 4.53 us
  local copies, waits for them, and re-layouts: 21 us -> 1.32 us
  other arithmetic: 10.8 us -> 0 us
  Pallas kernels: 0 us -> 8.7 us
  matrix products: 13.7 us -> 11.3 us
    all_to_all x0 -> x2, blocking collectives: none -> 119 us  [exchange(): block = lax.all_to_all(block, AXES, split_axis=0, concat_axis=0, tiled=True)]
    all_to_all x3 -> x0, waiting for transfers between devices: 102 us -> none  [the longest x1 51 us: shards(): lax.all_to_all(answered, ('tp', 'ep'), split_axis=0, concat_axis=0, tiled...]
    all_to_all x3 -> x0, starting transfers between devices: 28 us -> none  [the longest x1 11.2 us: shards(): lax.all_to_all(occupied, ('tp', 'ep'), split_axis=0, concat_axis=0, tiled...]
    ppermute x1, waiting for transfers between devices: 4.8 us -> 22.5 us  [shifted(): return lax.ppermute(block, axis, route)]
    gather x2 -> x0, local copies, waits for them, and re-layouts: 11.6 us -> none  [the longest x1 6.36 us: shards(): outgoing = with_blank[source_row].reshape(expert_count, capacity, features)]
    pallas_call x0 -> x2, Pallas kernels: none -> 8.7 us  [the longest x1 4.61 us: combine(): pl.pallas_call(functools.partial(combine_kernel, experts, cap), grid=(wid...]
    reduce_sum x4 -> x0, other arithmetic: 6.16 us -> none  [the longest x1 4.81 us: shards(): jnp.sum(weights[:, :, None] * picked.astype(jnp.float32), axis=1)]
    convert_element_type x2 -> x0, local copies, waits for them, and re-layouts: 3.49 us -> none  [the longest x1 3.39 us: shards(): picked.astype(jnp.float32)]
  transfers between devices with their start and end apart: 4 -> 1, of which waited for: 3 -> 1; matrix products, arithmetic and copies ran while one was open for 9% -> 0% of each run, Pallas kernels for 0% -> 0%
where the time goes in v1:
time: 168 us; the launch traced here: 167 us
  blocking collectives  119 us (71%)
  waiting for transfers between devices  22.5 us (13%)
  matrix products  11.3 us (7%)
  Pallas kernels  8.7 us (5%)
  starting transfers between devices  4.53 us (3%)
    all_to_all x2, blocking collectives, exchange(): block = lax.all_to_all(block, AXES, split_axis=0, concat_axis=0, tiled=True)  119 us
    ppermute x1, waiting for transfers between devices, shifted(): return lax.ppermute(block, axis, route)  22.5 us
    dot_general x1, matrix products, shards(): jnp.dot(hidden, down_proj[0, :, part], preferred_element_type=F32)  8.26 us
    pallas_call x1, Pallas kernels, combine(): pl.pallas_call(functools.partial(combine_kernel, experts, cap), grid=(wid...  4.61 us
    ppermute x1, starting transfers between devices, shifted(): return lax.ppermute(block, axis, route)  4.53 us
    pallas_call x1, Pallas kernels, dispatch(): pl.pallas_call(functools.partial(dispatch_kernel, experts // steps, cap),...  4.1 us
  transfers between devices with their start and end apart: 1, of which 1 were waited for; matrix products, arithmetic and copies ran while one was open for 0% of the time, Pallas kernels for 0%

profile of v1, /device:TPU:2, one launch (start us, length us, event | category | flops | bytes accessed | tf_op | source)
XLA Modules:
  0.0 167.3 jit_solution(17279312976161151734)
XLA Ops:
  0.0 0.0 copy-start
  0.0 4.5 %collective-permute-start = (bf16[1,128,2048]{2,1,0:T(8,128)(2,1)}, bf16[1,128,2048]{2,1,0:T(8,128)(2,1)}, u32[]{:S(2)}, u32[]{:S(2)}) collective-permute-start(bf16[1,128,2048]{2,1,0:T(8,128)(2,1)} %param.6), channel_id=1, source_target_pairs={{704,0},{0,64},{64,128},{128,192},{192,256},{256,320},{320,384},{3... | collective-permute-start | bytes 1572872 | tf_op jit(solution)/shard_map/ppermute | solution.py:18
  4.5 22.5 %collective-permute-done = bf16[1,128,2048]{2,1,0:T(8,128)(2,1)} collective-permute-done((bf16[1,128,2048]{2,1,0:T(8,128)(2,1)}, bf16[1,128,2048]{2,1,0:T(8,128)(2,1)}, u32[]{:S(2)}, u32[]{:S(2)}) %collective-permute-start) | collective-permute-done | bytes 524320 | tf_op jit(solution)/shard_map/ppermute | solution.py:18
  27.1 4.1 %dispatch.1 = bf16[512,2048]{1,0:T(8,128)(2,1)} custom-call(s32[2,128]{1,0:T(2,128)} %bitcast.40, bf16[128,2048]{1,0:T(8,128)(2,1)} %bitcast.5.x_ref), custom_call_target="tpu_custom_call" | custom-call | tf_op jit(solution)/shard_map/dispatch/pallas_call | solution.py:54
  31.2 0.0 copy-start.2
  31.2 62.2 %all_to_all.10 = bf16[64,8,2048]{2,1,0:T(8,128)(2,1)S(1)} all-to-all(bf16[64,8,2048]{2,1,0:T(8,128)(2,1)} %bitcast.39), channel_id=1, replica_groups=mesh['pp'=12,'tp'=16,'ep'=4] {'tp','ep'}, dimensions={0} | all-to-all | bytes 4194304 | tf_op jit(solution)/shard_map/all_to_all | solution.py:128
  93.3 0.0 copy-start.1
  93.3 1.3 copy-done.1
  94.6 0.0 copy-done.2
  94.6 3.0 %fusion.4 = f32[512,768]{1,0:T(8,128)} fusion(bf16[1,2048,768]{2,1,0:T(8,128)(2,1)S(1)} %copy-done.2, bf16[64,8,2048]{2,1,0:T(8,128)(2,1)S(1)} %all_to_all.10), kind=kOutput, calls=%fused_computation.4 | convolution fusion | flops 1610612736 | bytes 6815744 | tf_op jit(solution)/shard_map/dot_general | solution.py:144
  97.6 0.0 copy-done
  97.6 8.3 %fusion.9 = bf16[64,8,2048]{2,1,0:T(8,128)(2,1)} fusion(bf16[1,768,2048]{2,1,0:T(8,128)(2,1)S(1)} %copy-done, f32[512,768]{1,0:T(8,128)} %fusion.4, bf16[1,2048,768]{2,1,0:T(8,128)(2,1)} %param.10, bf16[64,8,2048]{2,1,0:T(8,128)(2,1)} %copy-done.1), kind=kOutput, calls=%fused_computation.7 | convolution fusion | flops 3224633344 | bytes 12058624 | tf_op jit(solution)/shard_map/dot_general | solution.py:151
  105.9 56.8 %all_to_all.11 = bf16[64,8,2048]{2,1,0:T(8,128)(2,1)} all-to-all(bf16[64,8,2048]{2,1,0:T(8,128)(2,1)} %fusion.9), channel_id=1, replica_groups=mesh['pp'=12,'tp'=16,'ep'=4] {'tp','ep'}, dimensions={0} | all-to-all | bytes 4194304 | tf_op jit(solution)/shard_map/all_to_all | solution.py:128
  162.7 4.6 %combine.1 = bf16[128,2048]{1,0:T(8,128)(2,1)} custom-call(s32[2,128]{1,0:T(2,128)} %bitcast.41, f32[2,128]{1,0:T(2,128)} %bitcast.42, bf16[512,2048]{1,0:T(8,128)(2,1)} %bitcast.38, bf16[128,2048]{1,0:T(8,128)(2,1)} %bitcast.5.x_ref), custom_call_target="tpu_custom_call" | custom-call | tf_op jit(solution)/shard_map/combine/pallas_call | solution.py:110
Async XLA Ops:
  0.0 97.6 %copy-start = (bf16[1,768,2048]{2,1,0:T(8,128)(2,1)S(1)}, bf16[1,768,2048]{2,1,0:T(8,128)(2,1)}, u32[]{:S(2)}) copy-start(bf16[1,768,2048]{2,1,0:T(8,128)(2,1)} %param.11) | copy-start | bytes 9437188
  0.0 27.1 %collective-permute-start = (bf16[1,128,2048]{2,1,0:T(8,128)(2,1)}, bf16[1,128,2048]{2,1,0:T(8,128)(2,1)}, u32[]{:S(2)}, u32[]{:S(2)}) collective-permute-start(bf16[1,128,2048]{2,1,0:T(8,128)(2,1)} %param.6), channel_id=1, source_target_pairs={{704,0},{0,64},{64,128},{128,192},{192,256},{256,320},{320,384},{3... | collective-permute-start | bytes 1572872 | tf_op jit(solution)/shard_map/ppermute | solution.py:18
  31.2 63.5 %copy-start.2 = (bf16[1,2048,768]{2,1,0:T(8,128)(2,1)S(1)}, bf16[1,2048,768]{2,1,0:T(8,128)(2,1)}, u32[]{:S(2)}) copy-start(bf16[1,2048,768]{2,1,0:T(8,128)(2,1)} %param.9) | copy-start | bytes 9437188
  93.3 1.3 copy-start.1

commit v2 on v1

v2 whole, which is shorter than its diff:
```python
import functools

import jax
import jax.numpy as jnp
from jax import lax
from jax.experimental import pallas as pl
from jax.experimental.pallas import tpu as pltpu
from jax.sharding import Mesh
from jax.sharding import PartitionSpec as P

SAME_CORE = ("y", "ep")
F32, BF16, I32 = jnp.float32, jnp.bfloat16, jnp.int32


def iota(shape, dim):
    return lax.broadcasted_iota(I32, shape, dim)


def moved(block, planes, swap):
    count, cores = lax.axis_size("pp"), lax.axis_size("core")
    route = []
    for p in range(count):
        for c in range(cores):
            to = ((p + planes) % count) * cores + (cores - 1 - c if swap else c)
            route.append((p * cores + c, to))
    return lax.ppermute(block, ("pp", "core"), route)


def route_kernel(width, core_ref, ids_ref, scores_ref, other_ref, own_ref):
    ids, scores = ids_ref[...], scores_ref[...]
    weights = scores / jnp.sum(scores, axis=0, keepdims=True)
    core = core_ref[0]
    half = (ids // width) % 2
    place = (ids // (2 * width)) * width + ids % width
    for ref, mine in ((other_ref, 1 - core), (own_ref, core)):
        ref[0:2, :] = jnp.where(half == mine, place, -1).astype(F32)
        ref[2:4, :] = weights


def route(ids, scores, width):
    core = lax.axis_index("core").astype(I32).reshape(1)
    shape = jax.ShapeDtypeStruct((4, ids.shape[1]), F32)
    vmem = pl.BlockSpec(memory_space=pltpu.VMEM)
    return pl.pallas_call(
        functools.partial(route_kernel, width),
        in_specs=[pl.BlockSpec(memory_space=pltpu.SMEM), vmem, vmem],
        out_specs=[vmem, vmem],
        out_shape=[shape, shape],
        name="route",
    )(core, ids, scores)


def dispatch_kernel(experts, cap, route_ref, x_ref, out_ref, normed_ref):
    step = pl.program_id(0)

    @pl.when(step == 0)
    def _():
        values = x_ref[...].astype(F32)
        scale = lax.rsqrt(jnp.mean(values * values, axis=1, keepdims=True) + 1e-06)
        normed_ref[...] = (values * scale).astype(BF16)

    names = route_ref[0:2, :].astype(I32)
    tokens = names.shape[1]
    place = step * experts + iota((experts, tokens), 0)
    member = (names[0:1, :] == place) | (names[1:2, :] == place)
    earlier = (iota((tokens, tokens), 0) < iota((tokens, tokens), 1)).astype(BF16)
    slot = jnp.dot(member.astype(BF16), earlier, preferred_element_type=F32).astype(I32)
    slot = jnp.where(member, slot, -1)
    pick = slot[:, None, :] == iota((experts, cap, tokens), 1)
    pick = pick.astype(F32).reshape(experts * cap, tokens).astype(BF16)
    out_ref[...] = jnp.dot(pick, normed_ref[...], preferred_element_type=F32).astype(BF16)


def dispatch(routed, arrived, experts, cap, steps=2):
    tokens, features = arrived.shape
    rows = experts * cap // steps
    return pl.pallas_call(
        functools.partial(dispatch_kernel, experts // steps, cap),
        grid=(steps,),
        in_specs=[
            pl.BlockSpec(routed.shape, lambda i: (0, 0)),
            pl.BlockSpec(arrived.shape, lambda i: (0, 0)),
        ],
        out_specs=pl.BlockSpec((rows, features), lambda i: (i, 0)),
        out_shape=jax.ShapeDtypeStruct((experts * cap, features), BF16),
        scratch_shapes=[pltpu.VMEM((tokens, features), BF16)],
        cost_estimate=pl.CostEstimate(
            flops=2 * experts * cap * tokens * features,
            bytes_accessed=2 * features * (tokens + experts * cap),
            transcendentals=0,
        ),
        name="dispatch",
    )(routed, arrived)


def combine_kernel(experts, cap, route_ref, back_ref, x_ref, out_ref, pick_ref, weight_ref):
    tokens = route_ref.shape[1]
    square = (tokens, tokens)

    @pl.when(pl.program_id(0) == 0)
    def _():
        column = lambda k: jnp.transpose(jnp.broadcast_to(route_ref[k : k + 1, :], square))
        names = [column(k).astype(I32) for k in range(2)]
        lane = iota(square, 1)
        member = ((names[0] == lane) | (names[1] == lane)).astype(BF16)
        earlier = (iota(square, 1) < iota(square, 0)).astype(BF16)
        slot = jnp.dot(earlier, member, preferred_element_type=F32)
        for k in range(2):
            mine = jnp.sum(jnp.where(names[k] == lane, slot, 0.0), axis=1, keepdims=True)
            at = names[k][:, 0:1] * cap + mine.astype(I32)
            here = (iota((tokens, experts * cap), 1) == at).astype(BF16)
            pick_ref[k * tokens : (k + 1) * tokens, :] = here
            weight_ref[k * tokens : (k + 1) * tokens, :] = column(2 + k)

    picked = jnp.dot(pick_ref[...], back_ref[...], preferred_element_type=F32)
    picked = picked * weight_ref[:, 0:1]
    total = x_ref[...].astype(F32) + (picked[:tokens] + picked[tokens:])
    out_ref[...] = total.astype(BF16)


def combine(routed, back, base, experts, cap, block=512):
    tokens, features = base.shape
    column = lambda rows: pl.BlockSpec((rows, block), lambda i: (0, i))
    return pl.pallas_call(
        functools.partial(combine_kernel, experts, cap),
        grid=(features // block,),
        in_specs=[
            pl.BlockSpec(routed.shape, lambda i: (0, 0)),
            column(experts * cap),
            column(tokens),
        ],
        out_specs=column(tokens),
        out_shape=jax.ShapeDtypeStruct((tokens, features), BF16),
        scratch_shapes=[
            pltpu.VMEM((2 * tokens, experts * cap), BF16),
            pltpu.VMEM((2 * tokens, tokens), F32),
        ],
        cost_estimate=pl.CostEstimate(
            flops=4 * experts * cap * tokens * features,
            bytes_accessed=2 * features * (2 * tokens + experts * cap),
            transcendentals=0,
        ),
        name="combine",
    )(routed, back, base)


def exchange(block, experts):
    shape = block.shape
    block = block.reshape(experts, -1, shape[1])
    block = lax.all_to_all(block, SAME_CORE, split_axis=0, concat_axis=0, tiled=True)
    return block.reshape(shape)


def expert_apply(tokens_in, gate_mat, up_mat, down_mat):
    gate_part = jnp.dot(tokens_in, gate_mat, preferred_element_type=F32)
    upward = jnp.dot(tokens_in, up_mat, preferred_element_type=F32)
    hidden = (jax.nn.silu(gate_part) * upward).astype(BF16)
    return jnp.dot(hidden, down_mat, preferred_element_type=F32).astype(BF16)


def shards(incoming, expert_ids, gate_scores, gate_proj, up_proj, down_proj):
    leaving = incoming[0]
    tokens, _ = leaving.shape
    columns = lax.axis_size("ep")
    experts = lax.axis_size("y") * columns
    cap = min(tokens, tokens * expert_ids.shape[2] // experts)
    weights = (gate_proj[0], up_proj[0], down_proj[0])
    other, own = route(expert_ids[0].T, gate_scores[0].T, columns)
    asked = moved(other, -1, True)
    swapped = moved(leaving, 0, True)
    arrived = moved(leaving, 1, False)
    first = dispatch(asked, swapped, experts, cap)
    first = exchange(first, experts)
    second = dispatch(own, arrived, experts, cap)
    second = exchange(second, experts)
    first = expert_apply(first, *weights)
    first = exchange(first, experts)
    second = expert_apply(second, *weights)
    second = exchange(second, experts)
    partial = combine(asked, first, swapped, experts, cap)
    partial = moved(partial, 1, True)
    out = combine(own, second, partial, experts, cap)
    return out[None]


def solution(mesh):
    planes, rows, columns = mesh.devices.shape
    devices = mesh.devices.reshape(planes, rows // 2, 2, columns)
    fine = Mesh(devices, ("pp", "y", "core", "ep"))
    spread = ("y", "core", "ep")
    placed = (P("pp", spread, None),) * 3 + (P(spread, None, None),) * 3
    return jax.shard_map(
        shards, mesh=fine, in_specs=placed, out_specs=P("pp", spread, None), check_vma=False
    )
```

time: 168 us -> 163 us (0.970)
  blocking collectives: 119 us -> 0 us
  waiting for transfers between devices: 22.5 us -> 78.9 us
  starting transfers between devices: 4.53 us -> 47.9 us
  matrix products: 11.3 us -> 19.2 us
  Pallas kernels: 8.7 us -> 15.7 us
    all_to_all x2 -> x0, blocking collectives: 119 us -> none  [exchange(): block = lax.all_to_all(block, AXES, split_axis=0, concat_axis=0, tiled=True)]
    all_to_all x0 -> x4, waiting for transfers between devices: none -> 62.3 us  [exchange(): lax.all_to_all(block, SAME_CORE, split_axis=0, concat_axis=0, tiled=True)]
    all_to_all x0 -> x4, starting transfers between devices: none -> 27.2 us  [exchange(): lax.all_to_all(block, SAME_CORE, split_axis=0, concat_axis=0, tiled=True)]
    ppermute x1 -> x4, starting transfers between devices: 4.53 us -> 20.7 us  [moved(): return lax.ppermute(block, ('pp', 'core'), route)]
    dot_general x2 -> x4, matrix products: 11.3 us -> 19.2 us  [the longest x2 11 us: expert_apply(): return jnp.dot(hidden, down_mat, preferred_element_type=F32).astype(BF16)]
    ppermute x1 -> x4, waiting for transfers between devices: 22.5 us -> 16.6 us  [moved(): return lax.ppermute(block, ('pp', 'core'), route)]
    pallas_call x1 -> x3, Pallas kernels: 4.61 us -> 9.87 us  [the longest x2 8.58 us: combine(): pl.pallas_call(functools.partial(combine_kernel, experts, cap), grid=(fea...]
    pallas_call x1 -> x2, Pallas kernels: 4.1 us -> 5.79 us  [dispatch(): pl.pallas_call(functools.partial(dispatch_kernel, experts // steps, cap),...]
  transfers between devices with their start and end apart: 1 -> 8, of which waited for: 1 -> 6; matrix products, arithmetic and copies ran while one was open for 0% -> 12% of each run, Pallas kernels for 0% -> 5%
where the time goes in v2:
time: 163 us; the launch traced here: 162 us
  waiting for transfers between devices  78.9 us (48%)
  starting transfers between devices  47.9 us (29%)
  matrix products  19.2 us (12%)
  Pallas kernels  15.7 us (10%)
    all_to_all x4, waiting for transfers between devices, exchange(): lax.all_to_all(block, SAME_CORE, split_axis=0, concat_axis=0, tiled=True)  62.3 us
    all_to_all x4, starting transfers between devices, exchange(): lax.all_to_all(block, SAME_CORE, split_axis=0, concat_axis=0, tiled=True)  27.2 us
    ppermute x4, starting transfers between devices, moved(): return lax.ppermute(block, ('pp', 'core'), route)  20.7 us
    ppermute x4, waiting for transfers between devices, moved(): return lax.ppermute(block, ('pp', 'core'), route)  16.6 us
    dot_general x2, matrix products, expert_apply(): return jnp.dot(hidden, down_mat, preferred_element_type=F32).astype(BF16)  11 us
    pallas_call x2, Pallas kernels, combine(): pl.pallas_call(functools.partial(combine_kernel, experts, cap), grid=(fea...  8.58 us
    dot_general x2, matrix products, expert_apply(): gate_part = jnp.dot(tokens_in, gate_mat, preferred_element_type=F32)  8.18 us
    pallas_call x2, Pallas kernels, dispatch(): pl.pallas_call(functools.partial(dispatch_kernel, experts // steps, cap),...  5.79 us
  transfers between devices with their start and end apart: 8, of which 6 were waited for; matrix products, arithmetic and copies ran while one was open for 12% of the time, Pallas kernels for 5%

profile of v2, /device:TPU:2, one launch (start us, length us, event | category | flops | bytes accessed | tf_op | source)
XLA Modules:
  0.0 162.3 jit_solution(15151538243616463232)
XLA Ops:
  0.0 2.2 %collective-permute-start.2 = (bf16[128,2048]{1,0:T(8,128)(2,1)}, bf16[128,2048]{1,0:T(8,128)(2,1)}, u32[]{:S(2)}, u32[]{:S(2)}) collective-permute-start(bf16[128,2048]{1,0:T(8,128)(2,1)} %bitcast.70), channel_id=1, source_target_pairs={{0,4},{4,0},{64,68},{68,64},{128,132},{132,128},{192,196},{196,192... | collective-permute-start | bytes 1572872 | tf_op jit(solution)/shard_map/ppermute | solution.py:26
  2.2 1.3 route.1
  3.5 14.7 %collective-permute-start.1 = (f32[4,128]{1,0:T(4,128)}, f32[4,128]{1,0:T(4,128)S(1)}, u32[]{:S(2)}, u32[]{:S(2)}) collective-permute-start(f32[4,128]{1,0:T(4,128)} %get-tuple-element.8), channel_id=1, source_target_pairs={{0,708},{4,704},{64,4},{68,0},{128,68},{132,64},{192,132},{196,128... | collective-permute-start | bytes 6152 | tf_op jit(solution)/shard_map/ppermute | solution.py:26
  18.2 1.5 collective-permute-done.1.route_ref
  19.7 0.6 copy-done.1
  20.3 2.9 %dispatch.3 = bf16[256,2048]{1,0:T(8,128)(2,1)} custom-call(f32[4,128]{1,0:T(4,128)} %copy-done.1, bf16[128,2048]{1,0:T(8,128)(2,1)} %collective-permute-done.2.x_ref), custom_call_target="tpu_custom_call" | custom-call | flops 134217728 | bytes 1572864 | tf_op jit(solution)/shard_map/dispatch/pallas_call | solution.py:77
  23.2 10.3 %all-to-all-start.2 = ((bf16[32,8,2048]{2,1,0:T(8,128)(2,1)}), bf16[32,8,2048]{2,1,0:T(8,128)(2,1)}, u32[]{:S(2)}, u32[]{:S(2)}) async-start(bf16[32,8,2048]{2,1,0:T(8,128)(2,1)} %bitcast.66), calls=%async_computation.2 | async-start | bytes 2097152 | tf_op jit(solution)/shard_map/all_to_all | solution.py:150
  33.5 1.9 %collective-permute-start = (bf16[128,2048]{1,0:T(8,128)(2,1)}, bf16[128,2048]{1,0:T(8,128)(2,1)}, u32[]{:S(2)}, u32[]{:S(2)}) collective-permute-start(bf16[128,2048]{1,0:T(8,128)(2,1)} %bitcast.71), channel_id=1, source_target_pairs={{0,64},{4,68},{64,128},{68,132},{128,192},{132,196},{192,256},{196... | collective-permute-start | bytes 1572872 | tf_op jit(solution)/shard_map/ppermute | solution.py:26
  35.4 15.1 %collective-permute-done.x_ref = bf16[128,2048]{1,0:T(8,128)(2,1)} collective-permute-done((bf16[128,2048]{1,0:T(8,128)(2,1)}, bf16[128,2048]{1,0:T(8,128)(2,1)}, u32[]{:S(2)}, u32[]{:S(2)}) %collective-permute-start) | collective-permute-done | bytes 524320 | tf_op jit(solution)/shard_map/ppermute | solution.py:26
  50.5 2.9 %dispatch.2 = bf16[256,2048]{1,0:T(8,128)(2,1)} custom-call(f32[4,128]{1,0:T(4,128)} %get-tuple-element.7.route_ref, bf16[128,2048]{1,0:T(8,128)(2,1)} %collective-permute-done.x_ref), custom_call_target="tpu_custom_call" | custom-call | flops 134217728 | bytes 1572864 | tf_op jit(solution)/shard_map/dispatch/pallas_call | solution.py:77
  53.4 7.8 %all-to-all-done.2 = bf16[32,8,2048]{2,1,0:T(8,128)(2,1)} async-done(((bf16[32,8,2048]{2,1,0:T(8,128)(2,1)}), bf16[32,8,2048]{2,1,0:T(8,128)(2,1)}, u32[]{:S(2)}, u32[]{:S(2)}) %all-to-all-start.2) | async-done | bytes 1048608 | tf_op jit(solution)/shard_map/all_to_all | solution.py:150
  61.2 5.6 %all-to-all-start = ((bf16[32,8,2048]{2,1,0:T(8,128)(2,1)}), bf16[32,8,2048]{2,1,0:T(8,128)(2,1)}, u32[]{:S(2)}, u32[]{:S(2)}) async-start(bf16[32,8,2048]{2,1,0:T(8,128)(2,1)} %bitcast.67), calls=%async_computation | async-start | bytes 2097152 | tf_op jit(solution)/shard_map/all_to_all | solution.py:150
  66.8 4.1 %fusion.8 = f32[256,768]{1,0:T(8,128)} fusion(bf16[1,2048,768]{2,1,0:T(8,128)(2,1)} %param.9, bf16[32,8,2048]{2,1,0:T(8,128)(2,1)} %all-to-all-done.2), kind=kOutput, calls=%fused_computation.8 | convolution fusion | flops 805306368 | bytes 4980736 | tf_op jit(solution)/shard_map/dot_general | solution.py:155
  70.9 5.5 %fusion.18 = bf16[32,8,2048]{2,1,0:T(8,128)(2,1)} fusion(bf16[1,768,2048]{2,1,0:T(8,128)(2,1)S(1)} %copy-done, bf16[1,2048,768]{2,1,0:T(8,128)(2,1)} %param.10, bf16[32,8,2048]{2,1,0:T(8,128)(2,1)} %all-to-all-done.2, f32[256,768]{1,0:T(8,128)} %fusion.8), kind=kOutput, calls=%fused_computation.14 | convolution fusion | flops 1612316672 | bytes 9175040 | tf_op jit(solution)/shard_map/dot_general | solution.py:158
  76.4 17.2 %all-to-all-done = bf16[32,8,2048]{2,1,0:T(8,128)(2,1)} async-done(((bf16[32,8,2048]{2,1,0:T(8,128)(2,1)}), bf16[32,8,2048]{2,1,0:T(8,128)(2,1)}, u32[]{:S(2)}, u32[]{:S(2)}) %all-to-all-start) | async-done | bytes 1048608 | tf_op jit(solution)/shard_map/all_to_all | solution.py:150
  93.7 5.6 %all-to-all-start.3 = ((bf16[32,8,2048]{2,1,0:T(8,128)(2,1)}), bf16[32,8,2048]{2,1,0:T(8,128)(2,1)}, u32[]{:S(2)}, u32[]{:S(2)}) async-start(bf16[32,8,2048]{2,1,0:T(8,128)(2,1)} %fusion.18), calls=%async_computation.3 | async-start | bytes 2097152 | tf_op jit(solution)/shard_map/all_to_all | solution.py:150
  99.3 4.1 %fusion.10 = f32[256,768]{1,0:T(8,128)} fusion(bf16[1,2048,768]{2,1,0:T(8,128)(2,1)} %param.9, bf16[32,8,2048]{2,1,0:T(8,128)(2,1)} %all-to-all-done), kind=kOutput, calls=%fused_computation.10 | convolution fusion | flops 805306368 | bytes 4980736 | tf_op jit(solution)/shard_map/dot_general | solution.py:155
  103.4 5.5 %fusion.21 = bf16[32,8,2048]{2,1,0:T(8,128)(2,1)} fusion(bf16[1,768,2048]{2,1,0:T(8,128)(2,1)S(1)} %copy-done, bf16[1,2048,768]{2,1,0:T(8,128)(2,1)} %param.10, bf16[32,8,2048]{2,1,0:T(8,128)(2,1)} %all-to-all-done, f32[256,768]{1,0:T(8,128)} %fusion.10), kind=kOutput, calls=%fused_computation.15 | convolution fusion | flops 1612316672 | bytes 9175040 | tf_op jit(solution)/shard_map/dot_general | solution.py:158
  108.9 17.0 %all-to-all-done.3 = bf16[32,8,2048]{2,1,0:T(8,128)(2,1)} async-done(((bf16[32,8,2048]{2,1,0:T(8,128)(2,1)}), bf16[32,8,2048]{2,1,0:T(8,128)(2,1)}, u32[]{:S(2)}, u32[]{:S(2)}) %all-to-all-start.3) | async-done | bytes 1048608 | tf_op jit(solution)/shard_map/all_to_all | solution.py:150
  125.8 5.6 %all-to-all-start.1 = ((bf16[32,8,2048]{2,1,0:T(8,128)(2,1)}), bf16[32,8,2048]{2,1,0:T(8,128)(2,1)}, u32[]{:S(2)}, u32[]{:S(2)}) async-start(bf16[32,8,2048]{2,1,0:T(8,128)(2,1)} %fusion.21), calls=%async_computation.1 | async-start | bytes 2097152 | tf_op jit(solution)/shard_map/all_to_all | solution.py:150
  131.5 4.3 %combine.2 = bf16[128,2048]{1,0:T(8,128)(2,1)} custom-call(f32[4,128]{1,0:T(4,128)} %copy-done.1, bf16[256,2048]{1,0:T(8,128)(2,1)} %bitcast.16.back_ref, bf16[128,2048]{1,0:T(8,128)(2,1)} %collective-permute-done.2.x_ref), custom_call_target="tpu_custom_call" | custom-call | flops 268435456 | bytes 2097152 | tf_op jit(solution)/shard_map/combine/pallas_call | solution.py:124
  135.7 1.9 %collective-permute-start.3 = (bf16[128,2048]{1,0:T(8,128)(2,1)}, bf16[128,2048]{1,0:T(8,128)(2,1)}, u32[]{:S(2)}, u32[]{:S(2)}) collective-permute-start(bf16[128,2048]{1,0:T(8,128)(2,1)} %combine.2), channel_id=1, source_target_pairs={{0,68},{4,64},{64,132},{68,128},{128,196},{132,192},{192,260},{196... | collective-permute-start | bytes 1572872 | tf_op jit(solution)/shard_map/ppermute | solution.py:26
  137.7 20.3 %all-to-all-done.1 = bf16[32,8,2048]{2,1,0:T(8,128)(2,1)} async-done(((bf16[32,8,2048]{2,1,0:T(8,128)(2,1)}), bf16[32,8,2048]{2,1,0:T(8,128)(2,1)}, u32[]{:S(2)}, u32[]{:S(2)}) %all-to-all-start.1) | async-done | bytes 1048608 | tf_op jit(solution)/shard_map/all_to_all | solution.py:150
  158.0 4.3 %combine.3 = bf16[128,2048]{1,0:T(8,128)(2,1)} custom-call(f32[4,128]{1,0:T(4,128)} %get-tuple-element.7.route_ref, bf16[256,2048]{1,0:T(8,128)(2,1)} %bitcast.12.back_ref, bf16[128,2048]{1,0:T(8,128)(2,1)} %collective-permute-done.3.x_ref), custom_call_target="tpu_custom_call" | custom-call | flops 268435456 | bytes 2097152 | tf_op jit(solution)/shard_map/combine/pallas_call | solution.py:124
  (5 shorter events, 0.0 us)
Async XLA Ops:
  0.0 70.9 %copy-start = (bf16[1,768,2048]{2,1,0:T(8,128)(2,1)S(1)}, bf16[1,768,2048]{2,1,0:T(8,128)(2,1)}, u32[]{:S(2)}) copy-start(bf16[1,768,2048]{2,1,0:T(8,128)(2,1)} %param.11) | copy-start | bytes 9437188
  0.0 19.7 %collective-permute-start.2 = (bf16[128,2048]{1,0:T(8,128)(2,1)}, bf16[128,2048]{1,0:T(8,128)(2,1)}, u32[]{:S(2)}, u32[]{:S(2)}) collective-permute-start(bf16[128,2048]{1,0:T(8,128)(2,1)} %bitcast.70), channel_id=1, source_target_pairs={{0,4},{4,0},{64,68},{68,64},{128,132},{132,128},{192,196},{196,192... | collective-permute-start | bytes 1572872 | tf_op jit(solution)/shard_map/ppermute | solution.py:26
  3.5 16.2 %collective-permute-start.1 = (f32[4,128]{1,0:T(4,128)}, f32[4,128]{1,0:T(4,128)S(1)}, u32[]{:S(2)}, u32[]{:S(2)}) collective-permute-start(f32[4,128]{1,0:T(4,128)} %get-tuple-element.8), channel_id=1, source_target_pairs={{0,708},{4,704},{64,4},{68,0},{128,68},{132,64},{192,132},{196,128... | collective-permute-start | bytes 6152 | tf_op jit(solution)/shard_map/ppermute | solution.py:26
  19.7 0.6 copy-start.1
  23.2 38.0 %all-to-all-start.2 = ((bf16[32,8,2048]{2,1,0:T(8,128)(2,1)}), bf16[32,8,2048]{2,1,0:T(8,128)(2,1)}, u32[]{:S(2)}, u32[]{:S(2)}) async-start(bf16[32,8,2048]{2,1,0:T(8,128)(2,1)} %bitcast.66), calls=%async_computation.2 | async-start | bytes 2097152 | tf_op jit(solution)/shard_map/all_to_all | solution.py:150
  33.5 17.1 %collective-permute-start = (bf16[128,2048]{1,0:T(8,128)(2,1)}, bf16[128,2048]{1,0:T(8,128)(2,1)}, u32[]{:S(2)}, u32[]{:S(2)}) collective-permute-start(bf16[128,2048]{1,0:T(8,128)(2,1)} %bitcast.71), channel_id=1, source_target_pairs={{0,64},{4,68},{64,128},{68,132},{128,192},{132,196},{192,256},{196... | collective-permute-start | bytes 1572872 | tf_op jit(solution)/shard_map/ppermute | solution.py:26
  61.2 32.5 %all-to-all-start = ((bf16[32,8,2048]{2,1,0:T(8,128)(2,1)}), bf16[32,8,2048]{2,1,0:T(8,128)(2,1)}, u32[]{:S(2)}, u32[]{:S(2)}) async-start(bf16[32,8,2048]{2,1,0:T(8,128)(2,1)} %bitcast.67), calls=%async_computation | async-start | bytes 2097152 | tf_op jit(solution)/shard_map/all_to_all | solution.py:150
  93.7 32.2 %all-to-all-start.3 = ((bf16[32,8,2048]{2,1,0:T(8,128)(2,1)}), bf16[32,8,2048]{2,1,0:T(8,128)(2,1)}, u32[]{:S(2)}, u32[]{:S(2)}) async-start(bf16[32,8,2048]{2,1,0:T(8,128)(2,1)} %fusion.18), calls=%async_computation.3 | async-start | bytes 2097152 | tf_op jit(solution)/shard_map/all_to_all | solution.py:150
  125.8 32.2 %all-to-all-start.1 = ((bf16[32,8,2048]{2,1,0:T(8,128)(2,1)}), bf16[32,8,2048]{2,1,0:T(8,128)(2,1)}, u32[]{:S(2)}, u32[]{:S(2)}) async-start(bf16[32,8,2048]{2,1,0:T(8,128)(2,1)} %fusion.21), calls=%async_computation.1 | async-start | bytes 2097152 | tf_op jit(solution)/shard_map/all_to_all | solution.py:150
  135.7 22.3 %collective-permute-start.3 = (bf16[128,2048]{1,0:T(8,128)(2,1)}, bf16[128,2048]{1,0:T(8,128)(2,1)}, u32[]{:S(2)}, u32[]{:S(2)}) collective-permute-start(bf16[128,2048]{1,0:T(8,128)(2,1)} %combine.2), channel_id=1, source_target_pairs={{0,68},{4,64},{64,132},{68,128},{128,196},{132,192},{192,260},{196... | collective-permute-start | bytes 1572872 | tf_op jit(solution)/shard_map/ppermute | solution.py:26
